TPU v7x, 32 devices: a whole 2x2x4 slice. The times are simulated.
32 devices in a mesh: dp: 4 (over x, core), mp: 8 (over z, y).
Axes of the slice: x: 2, y: 2, z: 4, core: 2. Of those that a mesh axis runs over, the one named last changes fastest.
Arguments:
- tokens: bfloat16 [25088, 512], P(('dp', 'mp')), may hold values from -6 to 6
- cotangent: bfloat16 [25088, 512], P(('dp', 'mp')), may hold values from -6 to 6
- image_counts: int32 [4], replicated, may hold values from 1 to 32, 96 in all
- params: float32 [8, 394324], P('mp', 'dp'), may hold values from -4 to 4, as said below
- moment_one: float32 [8, 394324], P('mp', 'dp'), may hold values from -96 to 96
- moment_two: float32 [8, 394324], P('mp', 'dp'), may hold values from 0 to 40, as said below
Outputs:
- output: bfloat16 [25088, 512], P(('dp', 'mp'))
- input_grad: bfloat16 [25088, 512], P(('dp', 'mp'))
- param_grad: float32 [8, 394324], P('mp', 'dp')
- new_params: float32 [8, 394324], P('mp', 'dp')
- revised_first_mean: float32 [8, 394324], P('mp', 'dp')
- new_moment_two: float32 [8, 394324], P('mp', 'dp')
Inputs may be any that keep to these rules, and one draw needn't show every extreme that they name: `image_counts`: the live images of a group are its first slots; the counts add up to three quarters of all slots, rounded down, and one group is full. `params`: laid out as its meaning says. `moment_two`: Positive, laid out as params.
All inputs are finite; a program needn't handle non-finite values.
Results may differ from a plain program's by a relative error of at most 0.022.
Values may be sent and summed in bfloat16 or wider, within the bound.
A program may use at most 192 MiB of HBM per device.

v0:
```python
import math
import jax
import jax.numpy as jnp
from jax import lax
from jax.sharding import PartitionSpec as P

C = 512
FF = 2048
HD = 32
WIN = 7
MAP = 14
SHIFT = 3
norm_eps = 1e-05
mask_fill = -100.0
learn_rate = 0.05
beta_one = 0.9
second_decay_rate = 0.999
adam_eps = 1e-08
weight_decay = 0.05
adam_step = 2.0
small_labels = ["norm1_gain", "norm1_bias", "proj_bias", "norm2_gain", "norm2_bias", "fc2_bias"]


def combine_rule(spec, left, right):
    return jnp.einsum(spec, left, right, preferred_element_type=jnp.float32)


def contract_rows(left, right):
    return lax.dot_general(
        left, right, (((0,), (0,)), ((), ())), preferred_element_type=jnp.float32
    )


def contract_cols(left, right):
    return lax.dot_general(
        left, right, (((1,), (1,)), ((), ())), preferred_element_type=jnp.float32
    )


def segment_shapes(width_rank, hidden_rank):
    span = 2 * WIN - 1
    return [
        ("qkv_weight", (C, 3 * width_rank)),
        ("proj_weight", (width_rank, C)),
        ("fc1_weight", (C, hidden_rank)),
        ("fc2_weight", (hidden_rank, C)),
        ("norm1_gain", (width_rank,)),
        ("norm1_bias", (width_rank,)),
        ("query_bias", (width_rank,)),
        ("value_bias", (width_rank,)),
        ("proj_bias", (width_rank,)),
        ("norm2_gain", (width_rank,)),
        ("norm2_bias", (width_rank,)),
        ("fc1_bias", (hidden_rank,)),
        ("fc2_bias", (width_rank,)),
        ("table", (span * span, width_rank // HD)),
    ]


def unpack(flat, width_rank, hidden_rank):
    groups = flat.shape[0]
    owner_pieces = {}
    offset = 0
    for label, shape in segment_shapes(width_rank, hidden_rank):
        amount = math.prod(shape)
        owner_pieces[label] = flat[:, offset : offset + amount].reshape((groups,) + shape)
        offset = offset + amount
    return owner_pieces


def pack(owner_pieces, width_rank, hidden_rank, length):
    groups = owner_pieces["qkv_weight"].shape[0]
    parts = [
        owner_pieces[label].reshape(groups, -1)
        for label, shape in segment_shapes(width_rank, hidden_rank)
    ]
    used = sum((part.shape[1] for part in parts))
    parts.append(jnp.zeros((groups, length - used), jnp.float32))
    return jnp.concatenate(parts, axis=1)


def window_tables():
    side = MAP // WIN
    span = 2 * WIN - 1
    inner = jnp.arange(WIN * WIN, dtype=jnp.int32)
    row_in = inner // WIN
    col_in = inner % WIN
    offset_index = (row_in[:, None] - row_in[None, :] + WIN - 1) * span + (
        col_in[:, None] - col_in[None, :] + WIN - 1
    )
    one_hot = (
        offset_index.reshape(-1)[:, None] == jnp.arange(span * span, dtype=jnp.int32)[None, :]
    ).astype(jnp.float32)
    window_ids = jnp.arange(side * side, dtype=jnp.int32)
    row_coord = (window_ids // side)[:, None] * WIN + row_in[None, :]
    col_coord = (window_ids % side)[:, None] * WIN + col_in[None, :]

    def region(coord):
        return (coord >= MAP - WIN).astype(jnp.int32) + (coord >= MAP - SHIFT).astype(jnp.int32)

    region_ids = region(row_coord) * 3 + region(col_coord)
    mask = jnp.where(region_ids[:, :, None] == region_ids[:, None, :], 0.0, mask_fill).astype(
        jnp.float32
    )
    return (one_hot, mask)


def to_windows(raster):
    width = raster.shape[-1]
    side = MAP // WIN
    grid = raster.reshape(-1, MAP, MAP, width)
    grid = jnp.roll(grid, (-SHIFT, -SHIFT), (1, 2))
    grid = grid.reshape(-1, side, WIN, side, WIN, width).transpose(0, 1, 3, 2, 4, 5)
    return grid.reshape(-1, side * side, WIN * WIN, width)


def from_windows(blocks):
    width = blocks.shape[-1]
    side = MAP // WIN
    grid = blocks.reshape(-1, side, side, WIN, WIN, width).transpose(0, 1, 3, 2, 4, 5)
    grid = grid.reshape(-1, MAP, MAP, width)
    grid = jnp.roll(grid, (SHIFT, SHIFT), (1, 2))
    return grid.reshape(-1, width)


def norm_stats(values):
    center = jnp.mean(values, axis=1, keepdims=True)
    spread = jnp.mean(jnp.square(values - center), axis=1, keepdims=True)
    return (center, lax.rsqrt(spread + norm_eps))


def norm_back(scaled, unit, scale):
    return scale * (
        scaled
        - jnp.mean(scaled, axis=1, keepdims=True)
        - unit * jnp.mean(scaled * unit, axis=1, keepdims=True)
    )


def gelu(values):
    return values * (0.5 * (1.0 + lax.erf(values * (1.0 / math.sqrt(2.0)))))


def gelu_derivative(values):
    cdf = 0.5 * (1.0 + lax.erf(values * (1.0 / math.sqrt(2.0))))
    density = jnp.exp(-0.5 * values * values) * (1.0 / math.sqrt(2.0 * math.pi))
    return cdf + values * density


def qkv_finish(raw, query_bias, value_bias):
    shift = jnp.stack([query_bias, jnp.zeros_like(query_bias), value_bias], axis=1)
    factor = jnp.array([HD ** (-0.5), 1.0, 1.0], jnp.float32)[None, None, :, None]
    return ((raw + shift[None]) * factor).astype(jnp.bfloat16)


def window_scores(blocks, table, one_hot, mask):
    heads = table.shape[1]
    size = WIN * WIN
    bias = (
        jnp.dot(one_hot, table, precision=lax.Precision.HIGHEST)
        .reshape(size, size, heads)
        .transpose(2, 0, 1)
    )
    scores = combine_rule("nwphd,nwqhd->nwhpq", blocks[:, :, :, :, 0, :], blocks[:, :, :, :, 1, :])
    return scores + bias[None, None] + mask[None, :, None]


def attend_forward(projected, table, one_hot, mask):
    heads = table.shape[1]
    blocks = to_windows(projected)
    count, wins = (blocks.shape[0], blocks.shape[1])
    blocks = blocks.reshape(count, wins, WIN * WIN, heads, 3, HD)
    scores = window_scores(blocks, table, one_hot, mask)
    top = jnp.max(scores, axis=-1, keepdims=True)
    log_total = top + jnp.log(jnp.sum(jnp.exp(scores - top), axis=-1, keepdims=True))
    soft = jnp.exp(scores - log_total).astype(jnp.bfloat16)
    mixed = combine_rule("nwhpq,nwqhd->nwphd", soft, blocks[:, :, :, :, 2, :]).astype(jnp.bfloat16)
    return (from_windows(mixed.reshape(count, wins, WIN * WIN, heads * HD)), log_total)


def attend_backward(projected, grad_mixed, table, log_total, one_hot, mask):
    heads = table.shape[1]
    size = WIN * WIN
    blocks = to_windows(projected)
    count, wins = (blocks.shape[0], blocks.shape[1])
    blocks = blocks.reshape(count, wins, size, heads, 3, HD)
    scores = window_scores(blocks, table, one_hot, mask)
    soft = jnp.exp(scores - log_total)
    incoming = to_windows(grad_mixed).reshape(count, wins, size, heads, HD)
    grad_value = combine_rule("nwhpq,nwphd->nwqhd", soft.astype(jnp.bfloat16), incoming)
    grad_soft = combine_rule("nwphd,nwqhd->nwhpq", incoming, blocks[:, :, :, :, 2, :])
    inner = jnp.sum(soft * grad_soft, axis=-1, keepdims=True)
    grad_scores = soft * (grad_soft - inner)
    grad_bias = jnp.sum(grad_scores, axis=(0, 1)).transpose(1, 2, 0).reshape(size * size, heads)
    grad_table = jnp.dot(one_hot.T, grad_bias, precision=lax.Precision.HIGHEST)
    rounded = grad_scores.astype(jnp.bfloat16)
    grad_query = combine_rule("nwhpq,nwqhd->nwphd", rounded, blocks[:, :, :, :, 1, :]) * HD ** (
        -0.5
    )
    grad_key = combine_rule("nwhpq,nwphd->nwqhd", rounded, blocks[:, :, :, :, 0, :])
    stacked = jnp.stack([grad_query, grad_key, grad_value], axis=4).reshape(
        count, wins, size, heads * 3 * HD
    )
    return (from_windows(stacked), grad_table)


def head_block(tokens, cotangent, live, live_all, owner_pieces, rank, one_hot, mask):
    ranks = lax.axis_size("mp")
    width_rank = owner_pieces["proj_weight"].shape[1]
    heads = width_rank // HD
    rows = tokens.shape[0]

    def linear_entries_arg(label):
        return owner_pieces[label][0].astype(jnp.float32)

    live_col = live[:, None]
    smalls = jnp.stack([owner_pieces[label][0] for label in small_labels])
    whole, cot_all, smalls_all = (
        lax.all_gather(tokens, "mp", axis=0, tiled=True),
        lax.all_gather(cotangent, "mp", axis=0, tiled=True),
        lax.all_gather(smalls, "mp", axis=1, tiled=True),
    )
    full = smalls_all.astype(jnp.float32)
    inputs_all = whole.astype(jnp.float32)
    center1, scale1 = norm_stats(inputs_all)
    unit1 = (inputs_all - center1) * scale1
    normed1 = (unit1 * full[0] + full[1]).astype(jnp.bfloat16)
    group_rows = whole.shape[0]
    raw = jnp.dot(
        normed1, owner_pieces["qkv_weight"][0], preferred_element_type=jnp.float32
    ).reshape(group_rows, heads, 3, HD)
    projected = qkv_finish(
        raw,
        linear_entries_arg("query_bias").reshape(heads, HD),
        linear_entries_arg("value_bias").reshape(heads, HD),
    )
    projected = projected.reshape(group_rows, heads * 3 * HD)
    table = owner_pieces["table"][0].astype(jnp.float32)
    mixed, log_total = attend_forward(projected, table, one_hot, mask)
    partial_value = jnp.dot(
        mixed, owner_pieces["proj_weight"][0], preferred_element_type=jnp.float32
    )
    attended = (
        lax.psum_scatter(
            partial_value.astype(jnp.bfloat16), "mp", scatter_dimension=0, tiled=True
        ).astype(jnp.float32)
        + full[2]
    )
    inputs = tokens.astype(jnp.float32)
    residual = inputs + attended
    center2, scale2 = norm_stats(residual)
    unit2 = (residual - center2) * scale2
    normed2 = (unit2 * full[3] + full[4]).astype(jnp.bfloat16)
    normed2_all = lax.all_gather(normed2, "mp", axis=0, tiled=True)
    hidden_before_gelu = jnp.dot(
        normed2_all, owner_pieces["fc1_weight"][0], preferred_element_type=jnp.float32
    ) + linear_entries_arg("fc1_bias")
    nonlinear_token_list = gelu(hidden_before_gelu).astype(jnp.bfloat16)
    feed_part = jnp.dot(
        nonlinear_token_list, owner_pieces["fc2_weight"][0], preferred_element_type=jnp.float32
    )
    perceptron_result = (
        lax.psum_scatter(
            feed_part.astype(jnp.bfloat16), "mp", scatter_dimension=0, tiled=True
        ).astype(jnp.float32)
        + full[5]
    )
    output = (live_col * (residual + perceptron_result)).astype(jnp.bfloat16)
    grad_out = live_col * cotangent.astype(jnp.float32)
    parameter_gradients = {}
    grad_all = cot_all * live_all[:, None].astype(jnp.bfloat16)
    parameter_gradients["fc2_weight"] = contract_rows(nonlinear_token_list, grad_all)[None]
    gradient_before_gelu = contract_cols(grad_all, owner_pieces["fc2_weight"][0]) * gelu_derivative(
        hidden_before_gelu
    )
    parameter_gradients["fc1_bias"] = jnp.sum(gradient_before_gelu, axis=0)[None]
    preact_rounded = gradient_before_gelu.astype(jnp.bfloat16)
    parameter_gradients["fc1_weight"] = contract_rows(normed2_all, preact_rounded)[None]
    grad_norm2 = lax.psum_scatter(
        contract_cols(preact_rounded, owner_pieces["fc1_weight"][0]).astype(jnp.bfloat16),
        "mp",
        scatter_dimension=0,
        tiled=True,
    ).astype(jnp.float32)
    grad_residual = grad_out + norm_back(grad_norm2 * full[3], unit2, scale2)
    residual_rounded = grad_residual.astype(jnp.bfloat16)
    rounded_all = lax.all_gather(residual_rounded, "mp", axis=0, tiled=True)
    parameter_gradients["proj_weight"] = contract_rows(mixed, rounded_all)[None]
    grad_mixed = contract_cols(rounded_all, owner_pieces["proj_weight"][0]).astype(jnp.bfloat16)
    grad_projected, grad_table = attend_backward(
        projected, grad_mixed, table, log_total, one_hot, mask
    )
    split = grad_projected.reshape(group_rows, heads, 3, HD)
    parameter_gradients["query_bias"] = jnp.sum(split[:, :, 0, :], axis=0).reshape(1, width_rank)
    parameter_gradients["value_bias"] = jnp.sum(split[:, :, 2, :], axis=0).reshape(1, width_rank)
    parameter_gradients["table"] = grad_table[None]
    projected_rounded = grad_projected.astype(jnp.bfloat16)
    parameter_gradients["qkv_weight"] = contract_rows(normed1, projected_rounded)[None]
    norm1_part = contract_cols(projected_rounded, owner_pieces["qkv_weight"][0])
    grad_norm1 = lax.psum_scatter(
        norm1_part.astype(jnp.bfloat16), "mp", scatter_dimension=0, tiled=True
    ).astype(jnp.float32)
    unit1_own = lax.dynamic_slice_in_dim(unit1, rank * rows, rows, 0)
    scale1_own = lax.dynamic_slice_in_dim(scale1, rank * rows, rows, 0)
    grad_input = (grad_residual + norm_back(grad_norm1 * full[0], unit1_own, scale1_own)).astype(
        jnp.bfloat16
    )
    small_terms = jnp.stack(
        [
            jnp.sum(grad_norm1 * unit1_own, axis=0),
            jnp.sum(grad_norm1, axis=0),
            jnp.sum(grad_residual, axis=0),
            jnp.sum(grad_norm2 * unit2, axis=0),
            jnp.sum(grad_norm2, axis=0),
            jnp.sum(grad_out, axis=0),
        ]
    ).reshape(len(small_labels), ranks, width_rank)
    small_sums = lax.psum_scatter(small_terms, "mp", scatter_dimension=1, tiled=True)
    for index, label in enumerate(small_labels):
        parameter_gradients[label] = small_sums[index]
    return (output, grad_input, parameter_gradients)


def local(tokens, cotangent, image_counts, params, moment_one, moment_two):
    ranks = lax.axis_size("mp")
    rank = lax.axis_index("mp")
    group = lax.axis_index("dp")
    width_rank = C // ranks
    hidden_rank = FF // ranks
    pixels = MAP * MAP
    rows = tokens.shape[0]
    shard_length = params.shape[1]
    one_hot, mask = window_tables()
    owned = lax.all_gather(params.astype(jnp.bfloat16), "dp", axis=1, tiled=True)
    limit = jnp.sum(
        jnp.where(jnp.arange(image_counts.shape[0], dtype=jnp.int32) == group, image_counts, 0)
    )
    images = rank * (rows // pixels) + jnp.arange(rows, dtype=jnp.int32) // pixels
    live = (images < limit).astype(jnp.float32)
    owner_pieces = unpack(owned, width_rank, hidden_rank)
    live_all = (jnp.arange(rows * ranks, dtype=jnp.int32) // pixels < limit).astype(jnp.float32)
    output, grad_input, parameter_gradients = head_block(
        tokens, cotangent, live, live_all, owner_pieces, rank, one_hot, mask
    )
    flat = pack(parameter_gradients, width_rank, hidden_rank, owned.shape[1])
    grad_shard = lax.psum_scatter(flat, "dp", scatter_dimension=1, tiled=True)
    weights_rank = (4 * C * C + 2 * C * FF) // ranks
    position = group * shard_length + jnp.arange(shard_length, dtype=jnp.int32)[None, :]
    decays = (position < weights_rank).astype(jnp.float32)
    new_one = beta_one * moment_one + (1.0 - beta_one) * grad_shard
    new_two = second_decay_rate * moment_two + (1.0 - second_decay_rate) * grad_shard * grad_shard
    corrected_one = new_one / (1.0 - beta_one**adam_step)
    corrected_two = new_two / (1.0 - second_decay_rate**adam_step)
    new_params = params - learn_rate * (
        corrected_one / (jnp.sqrt(corrected_two) + adam_eps) + weight_decay * decays * params
    )
    return (output, grad_input, grad_shard, new_params, new_one, new_two)


def solution(mesh):
    return jax.shard_map(
        local,
        mesh=mesh,
        in_specs=(
            P(("dp", "mp"), None),
            P(("dp", "mp"), None),
            P(),
            P("mp", "dp"),
            P("mp", "dp"),
            P("mp", "dp"),
        ),
        out_specs=(
            P(("dp", "mp"), None),
            P(("dp", "mp"), None),
            P("mp", "dp"),
            P("mp", "dp"),
            P("mp", "dp"),
            P("mp", "dp"),
        ),
        check_vma=False,
    )
```

profile of v0, /device:TPU:0, one launch (start us, length us, event | category | flops | bytes accessed | tf_op | source)
XLA Modules:
  0.0 1341.9 jit_solution(6521785367379511616)
XLA Ops:
  16.2 36.5 %all-reduce.6.cloned.1.call-done = bf16[394324]{0:T(1024)(128)(2,1)} async-done(((bf16[394324]{0:T(1024)(128)(2,1)}), bf16[394324]{0:T(1024)(128)(2,1)}) %all-reduce.6.cloned.1.call-update) | async-done | bytes 788664
  52.7 8.4 reshape.473
  61.5 27.7 %all-gather = bf16[8,64,6]{1,2,0:T(8,128)(2,1)S(1)} all-gather(bf16[1,64,6]{1,2,0:T(8,128)(2,1)S(1)} %bitcast.187), channel_id=1, replica_groups=mesh['dp'=4,'mp'=8] {'mp'}, dimensions={0}, use_global_device_ids=true | all-gather | bytes 6912 | tf_op jit(solution)/shard_map/all_gather | solution.py:221
  93.6 27.4 %all-gather.6.cloned.1.call-done = bf16[6272,512]{1,0:T(8,128)(2,1)} async-done(((bf16[784,512]{1,0:T(8,128)(2,1)}), bf16[6272,512]{1,0:T(8,128)(2,1)}) %all-gather.6.cloned.1.call-update) | async-done | bytes 6422544 | tf_op jit(solution)/shard_map/all_gather | solution.py:219
  121.0 3.9 convert_reduce_fusion
  128.7 5.7 fusion.4
  134.4 12.6 copy.83
  147.0 21.8 %reshape_reshape.20 = bf16[32,14,14,192]{3,2,1,0:T(8,128)(2,1)} reshape(bf16[6272,2,3,32]{3,2,1,0:T(4,128)(2,1)} %copy.83) | data formatting | bytes 4816896 | tf_op jit(solution)/shard_map/reshape;reshape | solution.py:111
  177.0 11.2 reshape_reshape.21
  188.2 25.3 %fusion.105 = (bf16[32,4,49,2,1,32]{5,4,3,0,2,1:T(2,128)(2,1)}, bf16[32,4,49,2,1,32]{5,4,3,0,2,1:T(2,128)(2,1)}, bf16[32,4,49,2,1,32]{5,4,3,0,2,1:T(2,128)(2,1)}) fusion(bf16[32,4,49,2,3,32]{5,4,3,0,2,1:T(4,128)(2,1)} %reshape_reshape.21), kind=kLoop, calls=%fused_computation.208 | loop fusion | bytes 4816896 | tf_op jit(solution)/shard_map/slice | solution.py:164
  213.5 12.7 copy.124
  226.3 14.0 %copy.123 = bf16[32,4,49,2,1,32]{2,5,3,1,0,4:T(8,128)(2,1)} copy(bf16[32,4,49,2,1,32]{5,4,3,0,2,1:T(2,128)(2,1)} %get-tuple-element.29) | data formatting | bytes 1605632
  240.3 13.9 %copy.125 = bf16[32,4,49,2,1,32]{2,5,3,1,0,4:T(8,128)(2,1)} copy(bf16[32,4,49,2,1,32]{5,4,3,0,2,1:T(2,128)(2,1)} %get-tuple-element.30) | data formatting | bytes 1605632
  254.2 3.8 fusion.14
  264.7 7.8 copy.92
  280.2 5.4 convolution_convert_fusion.3
  286.2 117.6 %reduce-scatter.7.cloned.1.call-done = bf16[784,512]{1,0:T(8,128)(2,1)} async-done(((bf16[6272,512]{1,0:T(8,128)(2,1)}), bf16[784,512]{1,0:T(8,128)(2,1)}) %reduce-scatter.7.cloned.1.call-update) | async-done | bytes 802832 | tf_op jit(solution)/shard_map/reduce_scatter | solution.py:244
  414.5 93.3 %all-gather.8.cloned.1.call-done = bf16[6272,512]{1,0:T(8,128)(2,1)} async-done(((bf16[784,512]{1,0:T(8,128)(2,1)}), bf16[6272,512]{1,0:T(8,128)(2,1)}) %all-gather.8.cloned.1.call-update) | async-done | bytes 6422544 | tf_op jit(solution)/shard_map/all_gather | solution.py:254
  507.9 6.6 multiply_convert_fusion
  514.5 93.9 %all-gather.10.cloned.1.call-done = bf16[6272,512]{1,0:T(8,128)(2,1)} async-done(((bf16[784,512]{1,0:T(8,128)(2,1)}), bf16[6272,512]{1,0:T(8,128)(2,1)}) %all-gather.10.cloned.1.call-update) | async-done | bytes 6422544 | tf_op jit(solution)/shard_map/all_gather | solution.py:220
  608.4 8.1 fusion.109
  616.5 4.5 convolution_convert_fusion.1
  621.1 6.5 convolution_convert_fusion.2
  628.5 110.6 %reduce-scatter.11.cloned.1.call-done = bf16[784,512]{1,0:T(8,128)(2,1)} async-done(((bf16[6272,512]{1,0:T(8,128)(2,1)}), bf16[784,512]{1,0:T(8,128)(2,1)}) %reduce-scatter.11.cloned.1.call-update) | async-done | bytes 802832 | tf_op jit(solution)/shard_map/reduce_scatter | solution.py:279
  741.8 120.0 %reduce-scatter.9.cloned.1.call-done = bf16[784,512]{1,0:T(8,128)(2,1)} async-done(((bf16[6272,512]{1,0:T(8,128)(2,1)}), bf16[784,512]{1,0:T(8,128)(2,1)}) %reduce-scatter.9.cloned.1.call-update) | async-done | bytes 802832 | tf_op jit(solution)/shard_map/reduce_scatter | solution.py:263
  869.0 9.1 fusion
  878.1 4.9 fusion.61
  884.3 5.1 fusion.64
  893.4 73.7 %all-gather.12.cloned.1.call-done = bf16[6272,512]{1,0:T(8,128)(2,1)} async-done(((bf16[784,512]{1,0:T(8,128)(2,1)}), bf16[6272,512]{1,0:T(8,128)(2,1)}) %all-gather.12.cloned.1.call-update) | async-done | bytes 6422544 | tf_op jit(solution)/shard_map/all_gather | solution.py:287
  967.1 4.9 convolution_convert_fusion.4
  979.2 8.8 copy.98
  988.1 7.9 convolution_bitcast_fusion
  1002.0 4.0 convolution_bitcast_fusion.1
  1009.2 10.6 pad_maximum_fusion
  1019.8 23.6 %copy.103 = f32[32,4,49,2,3,32]{5,4,3,0,2,1:T(4,128)} copy(f32[32,4,49,2,3,32]{2,5,3,1,0,4:T(8,128)} %pad_maximum_fusion) | data formatting | bytes 9633792 | tf_op jit(solution)/shard_map/stack | solution.py:201
  1043.3 26.9 %reshape_reshape.24 = f32[32,2,2,7,7,192]{5,0,4,3,2,1:T(8,128)} reshape(f32[32,4,49,2,3,32]{5,4,3,0,2,1:T(4,128)} %copy.103) | data formatting | bytes 9633792 | tf_op jit(solution)/shard_map/reshape;reshape | solution.py:120
  1074.9 3.7 fusion.9
  1084.6 3.7 copy.105
  1088.2 5.1 convert_element_type.224
  1093.4 4.6 convolution_convert_fusion
  1097.9 8.5 fusion.43
  1108.0 9.5 copy.107
  1117.6 24.9 %reshape_reshape.25 = f32[6272,2,3,32]{3,2,1,0:T(4,128)} reshape(f32[32,14,14,192]{3,2,1,0:T(8,128)} %copy.107) | data formatting | bytes 9633792 | tf_op jit(solution)/shard_map/reshape;reshape | solution.py:293
  1142.5 25.9 %slice_reduce_fusion = (f32[2,32]{1,0:T(2,128)S(1)}, f32[2,32]{1,0:T(2,128)S(1)}) fusion(f32[6272,2,3,32]{3,2,1,0:T(4,128)} %reshape_reshape.25), kind=kLoop, calls=%fused_computation.27 | loop fusion | flops 802688 | bytes 3211776 | tf_op jit(solution)/shard_map/reduce_sum | solution.py:295
  1172.1 63.5 %reduce-scatter.13.cloned.1.call-done = bf16[784,512]{1,0:T(8,128)(2,1)} async-done(((bf16[6272,512]{1,0:T(8,128)(2,1)}), bf16[784,512]{1,0:T(8,128)(2,1)}) %reduce-scatter.13.cloned.1.call-update) | async-done | bytes 802832 | tf_op jit(solution)/shard_map/reduce_scatter | solution.py:300
  1238.2 35.5 %all-reduce.1 = f32[6,8,64]{2,1,0:T(8,128)S(1)} all-reduce(f32[6,8,64]{2,1,0:T(8,128)S(1)} %constant_dynamic-update-slice_fusion), channel_id=6, replica_groups=mesh['dp'=4,'mp'=8] {'mp'}, use_global_device_ids=true, to_apply=%region_22.23.clone | all-reduce | flops 3072 | bytes 24576
  1292.3 37.1 %all-reduce.8.cloned.1.call-done = f32[1,394324]{1,0:T(1,128)} async-done(((f32[1,394324]{1,0:T(1,128)}), f32[1,394324]{1,0:T(1,128)}) %all-reduce.8.cloned.1.call-update) | async-done | bytes 1577312
  1329.4 4.9 multiply_subtract_fusion
  (274 shorter events, 118.4 us)
Async XLA Ops:
  8.0 44.7 %all-reduce.6.cloned.1.call-start = ((), (), s32[]{:S(2)}) async-start(), calls=%async_computation.12 | async-start | bytes 1581056
  15.2 105.8 %all-gather.6.cloned.1.call-start = ((), (), s32[]{:S(2)}) async-start(), calls=%async_computation.4 | async-start | bytes 7225344 | tf_op jit(solution)/shard_map/all_gather | solution.py:219
  15.8 388.0 %reduce-scatter.7.cloned.1.call-start = ((), (), s32[]{:S(2)}) async-start(), calls=%async_computation.5 | async-start | bytes 7225344 | tf_op jit(solution)/shard_map/reduce_scatter | solution.py:244
  16.1 75.5 %copy-start.39 = (s32[49,49]{1,0:T(8,128)}, s32[49,49]{1,0:T(8,128)S(1)}, u32[]{:S(2)}) copy-start(s32[49,49]{1,0:T(8,128)S(1)} %add_add_fusion.2) | copy-start | bytes 28816
  61.0 63.9 %copy-start.15 = (bf16[1,394324]{1,0:T(2,128)(2,1)}, bf16[1,394324]{1,0:T(2,128)(2,1)S(1)}, u32[]{:S(2)}) copy-start(bf16[1,394324]{1,0:T(2,128)(2,1)S(1)} %reshape.473) | copy-start | bytes 2365948
  90.5 170.2 %copy-start.22 = (f32[2,49,49]{1,2,0:T(8,128)}, f32[2,49,49]{1,2,0:T(8,128)S(1)}, u32[]{:S(2)}) copy-start(f32[2,49,49]{1,2,0:T(8,128)S(1)} %copy.90) | copy-start | bytes 57628
  92.9 35.7 %copy-start.25 = (bf16[512,192]{1,0:T(8,128)(2,1)}, bf16[512,192]{1,0:T(8,128)(2,1)S(1)}, u32[]{:S(2)}) copy-start(bf16[512,192]{1,0:T(8,128)(2,1)S(1)} %squeeze_reshape.19) | copy-start | bytes 589828
  93.6 35.0 %copy-start.43 = (f32[1,512]{1,0:T(1,128)}, f32[1,512]{1,0:T(1,128)S(1)}, u32[]{:S(2)}) copy-start(f32[1,512]{1,0:T(1,128)S(1)} %get-tuple-element.50) | copy-start | bytes 6148
  93.6 35.0 %copy-start.52 = (f32[1,512]{1,0:T(1,128)}, f32[1,512]{1,0:T(1,128)S(1)}, u32[]{:S(2)}) copy-start(f32[1,512]{1,0:T(1,128)S(1)} %get-tuple-element.49) | copy-start | bytes 6148
  125.7 8.8 copy-start.33
  226.3 27.9 %copy-start.6 = (bf16[32,4,49,2,1,32]{2,5,3,1,0,4:T(8,128)(2,1)}, bf16[32,4,49,2,1,32]{2,5,3,1,0,4:T(8,128)(2,1)S(1)}, u32[]{:S(2)}) copy-start(bf16[32,4,49,2,1,32]{2,5,3,1,0,4:T(8,128)(2,1)S(1)} %copy.124) | copy-start | bytes 2408452
  285.6 118.1 %copy-start.2 = (bf16[784,512]{1,0:T(8,128)(2,1)S(1)}, bf16[784,512]{1,0:T(8,128)(2,1)}, u32[]{:S(2)}) copy-start(bf16[784,512]{1,0:T(8,128)(2,1)} %param.7) | copy-start | bytes 2408452
  285.6 118.1 %copy-start.41 = (f32[1,512]{1,0:T(1,128)S(1)}, f32[1,512]{1,0:T(1,128)}, u32[]{:S(2)}) copy-start(f32[1,512]{1,0:T(1,128)} %get-tuple-element.48) | copy-start | bytes 6148
  285.6 121.3 %copy-start.42 = (f32[1,512]{1,0:T(1,128)S(1)}, f32[1,512]{1,0:T(1,128)}, u32[]{:S(2)}) copy-start(f32[1,512]{1,0:T(1,128)} %get-tuple-element.47) | copy-start | bytes 6148
  285.6 121.3 %copy-start.51 = (f32[1,512]{1,0:T(1,128)S(1)}, f32[1,512]{1,0:T(1,128)}, u32[]{:S(2)}) copy-start(f32[1,512]{1,0:T(1,128)} %get-tuple-element.46) | copy-start | bytes 6148
  285.7 123.5 %copy-start.55 = (s32[4]{0:T(128)S(1)}, s32[4]{0:T(128)}, u32[]{:S(2)}) copy-start(s32[4]{0:T(128)} %param.9) | copy-start | bytes 52
  285.7 124.8 %copy-start.16 = (bf16[1,394324]{1,0:T(2,128)(2,1)S(1)}, bf16[1,394324]{1,0:T(2,128)(2,1)}, u32[]{:S(2)}) copy-start(bf16[1,394324]{1,0:T(2,128)(2,1)} %copy-done.15) | copy-start | bytes 2365948
  285.7 222.2 %all-gather.8.cloned.1.call-start = ((), (), s32[]{:S(2)}) async-start(), calls=%async_computation.6 | async-start | bytes 7225344 | tf_op jit(solution)/shard_map/all_gather | solution.py:254
  408.4 200.0 %all-gather.10.cloned.1.call-start = ((), (), s32[]{:S(2)}) async-start(), calls=%async_computation.8 | async-start | bytes 7225344 | tf_op jit(solution)/shard_map/all_gather | solution.py:220
  409.1 330.0 %reduce-scatter.11.cloned.1.call-start = ((), (), s32[]{:S(2)}) async-start(), calls=%async_computation.9 | async-start | bytes 7225344 | tf_op jit(solution)/shard_map/reduce_scatter | solution.py:279
  414.4 100.0 %copy-start.28 = (bf16[512,256]{1,0:T(8,128)(2,1)}, bf16[512,256]{1,0:T(8,128)(2,1)S(1)}, u32[]{:S(2)}) copy-start(bf16[512,256]{1,0:T(8,128)(2,1)S(1)} %squeeze_reshape.22) | copy-start | bytes 786436
  608.4 8.1 copy-start.29
  621.0 240.8 %reduce-scatter.9.cloned.1.call-start = ((), (), s32[]{:S(2)}) async-start(), calls=%async_computation.7 | async-start | bytes 7225344 | tf_op jit(solution)/shard_map/reduce_scatter | solution.py:263
  627.6 234.2 %copy-start.50 = (f32[1,512]{1,0:T(1,128)S(1)}, f32[1,512]{1,0:T(1,128)}, u32[]{:S(2)}) copy-start(f32[1,512]{1,0:T(1,128)} %get-tuple-element.45) | copy-start | bytes 6148
  627.6 339.5 %all-gather.12.cloned.1.call-start = ((), (), s32[]{:S(2)}) async-start(), calls=%async_computation.10 | async-start | bytes 7225344 | tf_op jit(solution)/shard_map/all_gather | solution.py:287
  861.8 6.6 copy-start.56
  861.8 7.2 copy-start.34
  861.8 7.2 copy-start.37
  867.6 368.0 %reduce-scatter.13.cloned.1.call-start = ((), (), s32[]{:S(2)}) async-start(), calls=%async_computation.11 | async-start | bytes 7225344 | tf_op jit(solution)/shard_map/reduce_scatter | solution.py:300
  878.1 6.2 copy-start.17
  884.3 82.8 %copy-start.30 = (bf16[64,512]{1,0:T(8,128)(2,1)S(1)}, bf16[64,512]{1,0:T(8,128)(2,1)}, u32[]{:S(2)}) copy-start(bf16[64,512]{1,0:T(8,128)(2,1)} %squeeze_reshape.21) | copy-start | bytes 196612
  979.2 8.9 copy-start.19
  979.2 8.9 copy-start.23
  979.2 16.8 %slice-start = ((s8[7340032]{0:T(1024)(128)(4,1)}), s8[3145728]{0:T(1024)(128)(4,1)S(1)}, s32[]{:S(2)}) async-start(s8[7340032]{0:T(1024)(128)(4,1)} %bitcast.149), calls=%async_computation.14 | async-start | bytes 6291456
  988.1 7.9 slice-start.1
  988.1 7.9 copy-start.10
  988.1 7.9 copy-start.11
  1117.5 211.8 %all-reduce.8.cloned.1.call-start = ((), (), s32[]{:S(2)}) async-start(), calls=%async_computation.13 | async-start | bytes 3154944
  1142.5 26.1 %copy-start.31 = (f32[1,1,64,512]{3,1,2,0:T(1,128)S(1)}, f32[1,1,64,512]{3,1,2,0:T(1,128)}, u32[]{:S(2)}) copy-start(f32[1,1,64,512]{3,1,2,0:T(1,128)} %copy.126) | copy-start | bytes 393220
  1168.4 69.8 %copy-start.48 = (f32[1,8,64]{2,1,0:T(8,128)S(1)}, f32[1,8,64]{2,1,0:T(8,128)}, u32[]{:S(2)}) copy-start(f32[1,8,64]{2,1,0:T(8,128)} %stack.47) | copy-start | bytes 6148
  1168.4 69.8 %copy-start.46 = (f32[1,8,64]{2,1,0:T(8,128)S(1)}, f32[1,8,64]{2,1,0:T(8,128)}, u32[]{:S(2)}) copy-start(f32[1,8,64]{2,1,0:T(8,128)} %stack.48) | copy-start | bytes 6148
  1168.4 69.8 %copy-start.47 = (f32[1,8,64]{2,1,0:T(8,128)S(1)}, f32[1,8,64]{2,1,0:T(8,128)}, u32[]{:S(2)}) copy-start(f32[1,8,64]{2,1,0:T(8,128)} %stack.49) | copy-start | bytes 6148
  1168.4 69.8 %copy-start.45 = (f32[1,8,64]{2,1,0:T(8,128)S(1)}, f32[1,8,64]{2,1,0:T(8,128)}, u32[]{:S(2)}) copy-start(f32[1,8,64]{2,1,0:T(8,128)} %stack.50) | copy-start | bytes 6148
  1168.4 114.9 %copy-start.54 = (f32[256]{0:T(256)S(1)}, f32[256]{0:T(256)}, u32[]{:S(2)}) copy-start(f32[256]{0:T(256)} %get-tuple-element.59) | copy-start | bytes 3076
  1168.4 121.1 %copy-start.14 = (f32[784,512]{1,0:T(8,128)S(1)}, f32[784,512]{1,0:T(8,128)}, u32[]{:S(2)}) copy-start(f32[784,512]{1,0:T(8,128)} %copy-done.13) | copy-start | bytes 4816900
  1235.7 53.9 %copy-start.20 = (bf16[784,512]{1,0:T(8,128)(2,1)S(1)}, bf16[784,512]{1,0:T(8,128)(2,1)}, u32[]{:S(2)}) copy-start(bf16[784,512]{1,0:T(8,128)(2,1)} %reduce-scatter.13.cloned.1.call-done) | copy-start | bytes 2408452
  1238.0 91.4 %copy-start.27 = (f32[1,98581]{1,0:T(1,128)S(1)}, f32[1,98581]{1,0:T(1,128)}, u32[]{:S(2)}) copy-start(f32[1,98581]{1,0:T(1,128)} %param.10) | copy-start | bytes 1182976
  1238.0 91.4 %copy-start.32 = (f32[1,98581]{1,0:T(1,128)S(1)}, f32[1,98581]{1,0:T(1,128)}, u32[]{:S(2)}) copy-start(f32[1,98581]{1,0:T(1,128)} %param.11) | copy-start | bytes 1182976
  (24 other events, 84.9 us)
Sparse Core Ops, SparseCore 0:
  15.3 37.3 all-reduce.5
  1288.9 40.4 all-reduce.7
Sparse Core Ops, SparseCore 1:
  17.8 103.1 all-gather.5
  285.8 117.9 reduce-scatter.6
  408.4 99.4 all-gather.7
  510.1 98.3 all-gather.9
  621.1 117.9 reduce-scatter.10
  742.7 119.0 reduce-scatter.8
  867.7 99.4 all-gather.11
  1117.6 118.0 reduce-scatter.12
where the time goes:
time: 1350 us; the launch traced here: 1340 us
  waiting for transfers between devices  775 us (57%)
  local copies, waits for them, and re-layouts  298 us (22%)
  matrix products  94.2 us (7%)
  other arithmetic  92.8 us (7%)
  blocking collectives  63.2 us (5%)
  between operations  18.2 us (1%)
    reduce_scatter x1, waiting for transfers between devices, head_block(): lax.psum_scatter(feed_part.astype(jnp.bfloat16), 'mp', scatter_dimension=...  120 us
    reduce_scatter x1, waiting for transfers between devices, head_block(): lax.psum_scatter(partial_value.astype(jnp.bfloat16), 'mp', scatter_dimens...  118 us
    reduce_scatter x1, waiting for transfers between devices, head_block(): lax.psum_scatter(contract_cols(preact_rounded, owner_pieces['fc1_weight']...  111 us
    all_gather x1, waiting for transfers between devices, head_block(): lax.all_gather(cotangent, 'mp', axis=0, tiled=True)  93.9 us
    all_gather x1, waiting for transfers between devices, head_block(): normed2_all = lax.all_gather(normed2, 'mp', axis=0, tiled=True)  93.3 us
    unnamed x154, local copies, waits for them, and re-layouts  79.8 us
    unnamed x12, waiting for transfers between devices  74.9 us
    all_gather x1, waiting for transfers between devices, head_block(): rounded_all = lax.all_gather(residual_rounded, 'mp', axis=0, tiled=True)  73.7 us
  transfers between devices with their start and end apart: 10, of which 10 were waited for; matrix products, arithmetic and copies ran while one was open for 9% of the time, Pallas kernels for 0%

commit v1 on v0

--- a/solution.py
+++ b/solution.py
@@ -205,6 +205,28 @@
 
 
 def head_block(tokens, cotangent, live, live_all, owner_pieces, rank, one_hot, mask):
+
+    def pack_ways_over_axis(sheet, a_name):
+        p_next = jax.lax.psum(1, a_name)
+        f_next, latest, formed = (p_next, jax.lax.axis_index(a_name), sheet.shape[0])
+        chunks = [(j, (j + 1) % f_next) for j in range(f_next)]
+        by_rank = [(j, (j - 1) % f_next) for j in range(f_next)]
+        known = jnp.zeros((*sheet.shape[:0], f_next * formed, *sheet.shape[1:]), sheet.dtype)
+        known = lax.dynamic_update_slice_in_dim(known, sheet, latest * formed, axis=0)
+        a_now = carry_out = sheet
+        current_value = f_next // 2
+        for p in range(1, current_value + 1):
+            a_now = jax.lax.ppermute(a_now, a_name, chunks)
+            known = lax.dynamic_update_slice_in_dim(
+                known, a_now, (latest - p) % f_next * formed, axis=0
+            )
+            if p < f_next - current_value:
+                carry_out = jax.lax.ppermute(carry_out, a_name, by_rank)
+                known = lax.dynamic_update_slice_in_dim(
+                    known, carry_out, (latest + p) % f_next * formed, axis=0
+                )
+        return known
+
     ranks = lax.axis_size("mp")
     width_rank = owner_pieces["proj_weight"].shape[1]
     heads = width_rank // HD
@@ -251,7 +273,7 @@
     center2, scale2 = norm_stats(residual)
     unit2 = (residual - center2) * scale2
     normed2 = (unit2 * full[3] + full[4]).astype(jnp.bfloat16)
-    normed2_all = lax.all_gather(normed2, "mp", axis=0, tiled=True)
+    normed2_all = pack_ways_over_axis(normed2, "mp")
     hidden_before_gelu = jnp.dot(
         normed2_all, owner_pieces["fc1_weight"][0], preferred_element_type=jnp.float32
     ) + linear_entries_arg("fc1_bias")

time: 1350 us -> 1350 us (level)
  waiting for transfers between devices: 775 us -> 725 us
  starting transfers between devices: 1 us -> 29.9 us
  local copies, waits for them, and re-layouts: 298 us -> 314 us
    ppermute x0 -> x7, waiting for transfers between devices: none -> 135 us  [the longest x4 135 us: pack_ways_over_axis(): a_now = jax.lax.ppermute(a_now, a_name, chunks)]
    all_gather x1, waiting for transfers between devices: 93.9 us -> 0.01 us  [head_block(): lax.all_gather(cotangent, 'mp', axis=0, tiled=True)]
    all_gather x1 -> x0, waiting for transfers between devices: 93.3 us -> none  [head_block(): normed2_all = lax.all_gather(normed2, 'mp', axis=0, tiled=True)]
    ppermute x0 -> x7, starting transfers between devices: none -> 29 us  [the longest x3 20 us: pack_ways_over_axis(): carry_out = jax.lax.ppermute(carry_out, a_name, by_rank)]
    dynamic_update_slice x0 -> x7, local copies, waits for them, and re-layouts: none -> 13.5 us  [the longest x4 7.26 us: pack_ways_over_axis(): lax.dynamic_update_slice_in_dim(known, a_now, (latest - p) % f_next * for...]
    unnamed x12 -> x11, waiting for transfers between devices: 74.9 us -> 74.8 us
  transfers between devices with their start and end apart: 10 -> 16, of which waited for: 10 -> 12; matrix products, arithmetic and copies ran while one was open for 9% -> 10% of each run, Pallas kernels for 0% -> 0%
where the time goes in v1:
time: 1350 us; the launch traced here: 1340 us
  waiting for transfers between devices  725 us (54%)
  local copies, waits for them, and re-layouts  314 us (23%)
  matrix products  94.3 us (7%)
  other arithmetic  92.9 us (7%)
  blocking collectives  63.1 us (5%)
  starting transfers between devices  29.9 us (2%)
  between operations  18.4 us (1%)
    ppermute x4, waiting for transfers between devices, pack_ways_over_axis(): a_now = jax.lax.ppermute(a_now, a_name, chunks)  135 us
    reduce_scatter x1, waiting for transfers between devices, head_block(): lax.psum_scatter(feed_part.astype(jnp.bfloat16), 'mp', scatter_dimension=...  120 us
    reduce_scatter x1, waiting for transfers between devices, head_block(): lax.psum_scatter(partial_value.astype(jnp.bfloat16), 'mp', scatter_dimens...  117 us
    reduce_scatter x1, waiting for transfers between devices, head_block(): lax.psum_scatter(contract_cols(preact_rounded, owner_pieces['fc1_weight']...  113 us
    unnamed x154, local copies, waits for them, and re-layouts  79.8 us
    unnamed x11, waiting for transfers between devices  74.8 us
    all_gather x1, waiting for transfers between devices, head_block(): rounded_all = lax.all_gather(residual_rounded, 'mp', axis=0, tiled=True)  73.7 us
    reduce_scatter x1, waiting for transfers between devices, head_block(): lax.psum_scatter(norm1_part.astype(jnp.bfloat16), 'mp', scatter_dimension...  63.5 us
  transfers between devices with their start and end apart: 16, of which 12 were waited for; matrix products, arithmetic and copies ran while one was open for 10% of the time, Pallas kernels for 0%

profile of v1, /device:TPU:0, one launch (start us, length us, event | category | flops | bytes accessed | tf_op | source)
XLA Modules:
  0.0 1337.6 jit_solution(15934537453444347148)
XLA Ops:
  16.1 36.5 %all-reduce.6.cloned.1.call-done = bf16[394324]{0:T(1024)(128)(2,1)} async-done(((bf16[394324]{0:T(1024)(128)(2,1)}), bf16[394324]{0:T(1024)(128)(2,1)}) %all-reduce.6.cloned.1.call-update) | async-done | bytes 788664
  52.6 8.4 reshape.473
  61.5 27.7 %all-gather = bf16[8,64,6]{1,2,0:T(8,128)(2,1)S(1)} all-gather(bf16[1,64,6]{1,2,0:T(8,128)(2,1)S(1)} %bitcast.188), channel_id=1, replica_groups=mesh['dp'=4,'mp'=8] {'mp'}, dimensions={0}, use_global_device_ids=true | all-gather | bytes 6912 | tf_op jit(solution)/shard_map/all_gather | solution.py:243
  93.6 27.4 %all-gather.5.cloned.1.call-done = bf16[6272,512]{1,0:T(8,128)(2,1)} async-done(((bf16[784,512]{1,0:T(8,128)(2,1)}), bf16[6272,512]{1,0:T(8,128)(2,1)}) %all-gather.5.cloned.1.call-update) | async-done | bytes 6422544 | tf_op jit(solution)/shard_map/all_gather | solution.py:241
  121.0 3.9 convert_reduce_fusion
  128.6 5.8 fusion.4
  134.4 12.6 copy.83
  147.0 21.8 %reshape_reshape.20 = bf16[32,14,14,192]{3,2,1,0:T(8,128)(2,1)} reshape(bf16[6272,2,3,32]{3,2,1,0:T(4,128)(2,1)} %copy.83) | data formatting | bytes 4816896 | tf_op jit(solution)/shard_map/reshape;reshape | solution.py:111
  177.0 11.2 reshape_reshape.21
  188.2 25.3 %fusion.109 = (bf16[32,4,49,2,1,32]{5,4,3,0,2,1:T(2,128)(2,1)}, bf16[32,4,49,2,1,32]{5,4,3,0,2,1:T(2,128)(2,1)}, bf16[32,4,49,2,1,32]{5,4,3,0,2,1:T(2,128)(2,1)}) fusion(bf16[32,4,49,2,3,32]{5,4,3,0,2,1:T(4,128)(2,1)} %reshape_reshape.21), kind=kLoop, calls=%fused_computation.217 | loop fusion | bytes 4816896 | tf_op jit(solution)/shard_map/slice | solution.py:164
  213.5 12.7 copy.124
  226.2 14.0 %copy.123 = bf16[32,4,49,2,1,32]{2,5,3,1,0,4:T(8,128)(2,1)} copy(bf16[32,4,49,2,1,32]{5,4,3,0,2,1:T(2,128)(2,1)} %get-tuple-element.31) | data formatting | bytes 1605632
  240.2 14.1 %copy.125 = bf16[32,4,49,2,1,32]{2,5,3,1,0,4:T(8,128)(2,1)} copy(bf16[32,4,49,2,1,32]{5,4,3,0,2,1:T(2,128)(2,1)} %get-tuple-element.32) | data formatting | bytes 1605632
  264.9 7.8 copy.92
  280.4 5.4 convolution_convert_fusion.3
  286.7 117.3 %reduce-scatter.7.cloned.1.call-done = bf16[784,512]{1,0:T(8,128)(2,1)} async-done(((bf16[6272,512]{1,0:T(8,128)(2,1)}), bf16[784,512]{1,0:T(8,128)(2,1)}) %reduce-scatter.7.cloned.1.call-update) | async-done | bytes 802832 | tf_op jit(solution)/shard_map/reduce_scatter | solution.py:266
  416.5 38.9 %collective-permute-done = bf16[784,512]{1,0:T(8,128)(2,1)S(1)} collective-permute-done((bf16[784,512]{1,0:T(8,128)(2,1)S(1)}, bf16[784,512]{1,0:T(8,128)(2,1)S(1)}, u32[]{:S(2)}, u32[]{:S(2)}) %collective-permute-start) | collective-permute-done | bytes 802848 | tf_op jit(solution)/shard_map/ppermute | solution.py:219
  460.1 47.2 %collective-permute-done.2 = bf16[784,512]{1,0:T(8,128)(2,1)} collective-permute-done((bf16[784,512]{1,0:T(8,128)(2,1)S(1)}, bf16[784,512]{1,0:T(8,128)(2,1)}, u32[]{:S(2)}, u32[]{:S(2)}) %collective-permute-start.2) | collective-permute-done | bytes 802848 | tf_op jit(solution)/shard_map/ppermute | solution.py:219
  514.2 14.5 %collective-permute-start.5 = (bf16[784,512]{1,0:T(8,128)(2,1)}, bf16[784,512]{1,0:T(8,128)(2,1)}, u32[]{:S(2)}, u32[]{:S(2)}) collective-permute-start(bf16[784,512]{1,0:T(8,128)(2,1)} %collective-permute-done.3), channel_id=1, source_target_pairs={{0,7},{1,0},{2,1},{3,2},{4,3},{5,4},{6,5},{7,6},{8,15},{9,8},{10,9... | collective-permute-start | bytes 2408456 | tf_op jit(solution)/shard_map/ppermute | solution.py:224
  528.7 30.7 %collective-permute-done.4 = bf16[784,512]{1,0:T(8,128)(2,1)} collective-permute-done((bf16[784,512]{1,0:T(8,128)(2,1)}, bf16[784,512]{1,0:T(8,128)(2,1)}, u32[]{:S(2)}, u32[]{:S(2)}) %collective-permute-start.4) | collective-permute-done | bytes 802848 | tf_op jit(solution)/shard_map/ppermute | solution.py:219
  574.4 18.3 %collective-permute-done.6 = bf16[784,512]{1,0:T(8,128)(2,1)} collective-permute-done((bf16[784,512]{1,0:T(8,128)(2,1)}, bf16[784,512]{1,0:T(8,128)(2,1)}, u32[]{:S(2)}, u32[]{:S(2)}) %collective-permute-start.6) | collective-permute-done | bytes 802848 | tf_op jit(solution)/shard_map/ppermute | solution.py:219
  594.7 6.6 multiply_convert_fusion
  601.3 8.0 fusion.113
  609.3 4.6 convolution_convert_fusion.1
  614.4 6.4 convolution_convert_fusion.2
  621.5 113.1 %reduce-scatter.11.cloned.1.call-done = bf16[784,512]{1,0:T(8,128)(2,1)} async-done(((bf16[6272,512]{1,0:T(8,128)(2,1)}), bf16[784,512]{1,0:T(8,128)(2,1)}) %reduce-scatter.11.cloned.1.call-update) | async-done | bytes 802832 | tf_op jit(solution)/shard_map/reduce_scatter | solution.py:301
  737.4 120.0 %reduce-scatter.9.cloned.1.call-done = bf16[784,512]{1,0:T(8,128)(2,1)} async-done(((bf16[6272,512]{1,0:T(8,128)(2,1)}), bf16[784,512]{1,0:T(8,128)(2,1)}) %reduce-scatter.9.cloned.1.call-update) | async-done | bytes 802832 | tf_op jit(solution)/shard_map/reduce_scatter | solution.py:285
  864.6 9.1 fusion
  873.7 4.9 fusion.65
  879.9 5.1 fusion.68
  889.0 73.7 %all-gather.9.cloned.1.call-done = bf16[6272,512]{1,0:T(8,128)(2,1)} async-done(((bf16[784,512]{1,0:T(8,128)(2,1)}), bf16[6272,512]{1,0:T(8,128)(2,1)}) %all-gather.9.cloned.1.call-update) | async-done | bytes 6422544 | tf_op jit(solution)/shard_map/all_gather | solution.py:309
  962.7 4.9 convolution_convert_fusion.4
  974.8 8.8 copy.98
  983.6 7.9 convolution_bitcast_fusion
  997.6 4.0 convolution_bitcast_fusion.1
  1004.7 10.6 pad_maximum_fusion
  1015.3 23.6 %copy.103 = f32[32,4,49,2,3,32]{5,4,3,0,2,1:T(4,128)} copy(f32[32,4,49,2,3,32]{2,5,3,1,0,4:T(8,128)} %pad_maximum_fusion) | data formatting | bytes 9633792 | tf_op jit(solution)/shard_map/stack | solution.py:201
  1038.9 26.7 %reshape_reshape.24 = f32[32,2,2,7,7,192]{5,0,4,3,2,1:T(8,128)} reshape(f32[32,4,49,2,3,32]{5,4,3,0,2,1:T(4,128)} %copy.103) | data formatting | bytes 9633792 | tf_op jit(solution)/shard_map/reshape;reshape | solution.py:120
  1083.7 5.1 convert_element_type.224
  1088.8 4.6 convolution_convert_fusion
  1093.4 8.6 fusion.47
  1103.5 9.5 copy.107
  1113.1 24.9 %reshape_reshape.25 = f32[6272,2,3,32]{3,2,1,0:T(4,128)} reshape(f32[32,14,14,192]{3,2,1,0:T(8,128)} %copy.107) | data formatting | bytes 9633792 | tf_op jit(solution)/shard_map/reshape;reshape | solution.py:315
  1138.0 25.9 %slice_reduce_fusion = (f32[2,32]{1,0:T(2,128)S(1)}, f32[2,32]{1,0:T(2,128)S(1)}) fusion(f32[6272,2,3,32]{3,2,1,0:T(4,128)} %reshape_reshape.25), kind=kLoop, calls=%fused_computation.27 | loop fusion | flops 802688 | bytes 3211776 | tf_op jit(solution)/shard_map/reduce_sum | solution.py:317
  1167.7 63.5 %reduce-scatter.13.cloned.1.call-done = bf16[784,512]{1,0:T(8,128)(2,1)} async-done(((bf16[6272,512]{1,0:T(8,128)(2,1)}), bf16[784,512]{1,0:T(8,128)(2,1)}) %reduce-scatter.13.cloned.1.call-update) | async-done | bytes 802832 | tf_op jit(solution)/shard_map/reduce_scatter | solution.py:322
  1233.7 35.5 %all-reduce.1 = f32[6,8,64]{2,1,0:T(8,128)S(1)} all-reduce(f32[6,8,64]{2,1,0:T(8,128)S(1)} %constant_dynamic-update-slice_fusion), channel_id=6, replica_groups=mesh['dp'=4,'mp'=8] {'mp'}, use_global_device_ids=true, to_apply=%region_22.23.clone | all-reduce | flops 3072 | bytes 24576
  1287.7 37.1 %all-reduce.8.cloned.1.call-done = f32[1,394324]{1,0:T(1,128)} async-done(((f32[1,394324]{1,0:T(1,128)}), f32[1,394324]{1,0:T(1,128)}) %all-reduce.8.cloned.1.call-update) | async-done | bytes 1577312
  1324.8 4.9 multiply_subtract_fusion
  (293 shorter events, 160.5 us)
Async XLA Ops:
  8.0 44.7 %all-reduce.6.cloned.1.call-start = ((), (), s32[]{:S(2)}) async-start(), calls=%async_computation.11 | async-start | bytes 1581056
  15.1 105.8 %all-gather.5.cloned.1.call-start = ((), (), s32[]{:S(2)}) async-start(), calls=%async_computation.4 | async-start | bytes 7225344 | tf_op jit(solution)/shard_map/all_gather | solution.py:241
  15.7 388.3 %reduce-scatter.7.cloned.1.call-start = ((), (), s32[]{:S(2)}) async-start(), calls=%async_computation.5 | async-start | bytes 7225344 | tf_op jit(solution)/shard_map/reduce_scatter | solution.py:266
  16.0 75.5 %copy-start.39 = (s32[49,49]{1,0:T(8,128)}, s32[49,49]{1,0:T(8,128)S(1)}, u32[]{:S(2)}) copy-start(s32[49,49]{1,0:T(8,128)S(1)} %add_add_fusion.2) | copy-start | bytes 28816
  61.0 63.9 %copy-start.15 = (bf16[1,394324]{1,0:T(2,128)(2,1)}, bf16[1,394324]{1,0:T(2,128)(2,1)S(1)}, u32[]{:S(2)}) copy-start(bf16[1,394324]{1,0:T(2,128)(2,1)S(1)} %reshape.473) | copy-start | bytes 2365948
  90.5 170.4 %copy-start.22 = (f32[2,49,49]{1,2,0:T(8,128)}, f32[2,49,49]{1,2,0:T(8,128)S(1)}, u32[]{:S(2)}) copy-start(f32[2,49,49]{1,2,0:T(8,128)S(1)} %copy.90) | copy-start | bytes 57628
  92.8 35.7 %copy-start.25 = (bf16[512,192]{1,0:T(8,128)(2,1)}, bf16[512,192]{1,0:T(8,128)(2,1)S(1)}, u32[]{:S(2)}) copy-start(bf16[512,192]{1,0:T(8,128)(2,1)S(1)} %squeeze_reshape.19) | copy-start | bytes 589828
  93.6 35.0 %copy-start.43 = (f32[1,512]{1,0:T(1,128)}, f32[1,512]{1,0:T(1,128)S(1)}, u32[]{:S(2)}) copy-start(f32[1,512]{1,0:T(1,128)S(1)} %get-tuple-element.52) | copy-start | bytes 6148
  93.6 35.0 %copy-start.52 = (f32[1,512]{1,0:T(1,128)}, f32[1,512]{1,0:T(1,128)S(1)}, u32[]{:S(2)}) copy-start(f32[1,512]{1,0:T(1,128)S(1)} %get-tuple-element.51) | copy-start | bytes 6148
  125.6 8.8 copy-start.33
  226.2 28.1 %copy-start.6 = (bf16[32,4,49,2,1,32]{2,5,3,1,0,4:T(8,128)(2,1)}, bf16[32,4,49,2,1,32]{2,5,3,1,0,4:T(8,128)(2,1)S(1)}, u32[]{:S(2)}) copy-start(bf16[32,4,49,2,1,32]{2,5,3,1,0,4:T(8,128)(2,1)S(1)} %copy.124) | copy-start | bytes 2408452
  285.8 118.2 %copy-start.2 = (bf16[784,512]{1,0:T(8,128)(2,1)S(1)}, bf16[784,512]{1,0:T(8,128)(2,1)}, u32[]{:S(2)}) copy-start(bf16[784,512]{1,0:T(8,128)(2,1)} %param.7) | copy-start | bytes 2408452
  285.8 118.2 %copy-start.41 = (f32[1,512]{1,0:T(1,128)S(1)}, f32[1,512]{1,0:T(1,128)}, u32[]{:S(2)}) copy-start(f32[1,512]{1,0:T(1,128)} %get-tuple-element.50) | copy-start | bytes 6148
  285.9 315.4 %all-gather.7.cloned.1.call-start = ((), (), s32[]{:S(2)}) async-start(), calls=%async_computation.7 | async-start | bytes 7225344 | tf_op jit(solution)/shard_map/all_gather | solution.py:242
  286.4 448.2 %reduce-scatter.11.cloned.1.call-start = ((), (), s32[]{:S(2)}) async-start(), calls=%async_computation.8 | async-start | bytes 7225344 | tf_op jit(solution)/shard_map/reduce_scatter | solution.py:301
  407.2 102.7 %copy-start.55 = (s32[4]{0:T(128)S(1)}, s32[4]{0:T(128)}, u32[]{:S(2)}) copy-start(s32[4]{0:T(128)} %param.9) | copy-start | bytes 52
  407.2 104.0 %copy-start.16 = (bf16[1,394324]{1,0:T(2,128)(2,1)S(1)}, bf16[1,394324]{1,0:T(2,128)(2,1)}, u32[]{:S(2)}) copy-start(bf16[1,394324]{1,0:T(2,128)(2,1)} %copy-done.15) | copy-start | bytes 2365948
  411.7 43.6 %collective-permute-start = (bf16[784,512]{1,0:T(8,128)(2,1)S(1)}, bf16[784,512]{1,0:T(8,128)(2,1)S(1)}, u32[]{:S(2)}, u32[]{:S(2)}) collective-permute-start(bf16[784,512]{1,0:T(8,128)(2,1)S(1)} %get-tuple-element.29), channel_id=1, source_target_pairs={{0,1},{1,2},{2,3},{3,4},{4,5},{5,6},{6,7},{7,0},{8,9},{9,10},{10,1... | collective-permute-start | bytes 2408456 | tf_op jit(solution)/shard_map/ppermute | solution.py:219
  413.2 44.6 %collective-permute-start.1 = (bf16[784,512]{1,0:T(8,128)(2,1)S(1)}, bf16[784,512]{1,0:T(8,128)(2,1)}, u32[]{:S(2)}, u32[]{:S(2)}) collective-permute-start(bf16[784,512]{1,0:T(8,128)(2,1)S(1)} %get-tuple-element.29), channel_id=1, source_target_pairs={{0,7},{1,0},{2,1},{3,2},{4,3},{5,4},{6,5},{7,6},{8,15},{9,8},{10,9... | collective-permute-start | bytes 2408456 | tf_op jit(solution)/shard_map/ppermute | solution.py:224
  455.3 52.0 %collective-permute-start.2 = (bf16[784,512]{1,0:T(8,128)(2,1)S(1)}, bf16[784,512]{1,0:T(8,128)(2,1)}, u32[]{:S(2)}, u32[]{:S(2)}) collective-permute-start(bf16[784,512]{1,0:T(8,128)(2,1)S(1)} %collective-permute-done), channel_id=1, source_target_pairs={{0,1},{1,2},{2,3},{3,4},{4,5},{5,6},{6,7},{7,0},{8,9},{9,10},{10,1... | collective-permute-start | bytes 2408456 | tf_op jit(solution)/shard_map/ppermute | solution.py:219
  457.8 56.4 %collective-permute-start.3 = (bf16[784,512]{1,0:T(8,128)(2,1)}, bf16[784,512]{1,0:T(8,128)(2,1)}, u32[]{:S(2)}, u32[]{:S(2)}) collective-permute-start(bf16[784,512]{1,0:T(8,128)(2,1)} %collective-permute-done.1), channel_id=1, source_target_pairs={{0,7},{1,0},{2,1},{3,2},{4,3},{5,4},{6,5},{7,6},{8,15},{9,8},{10,9... | collective-permute-start | bytes 2408456 | tf_op jit(solution)/shard_map/ppermute | solution.py:224
  507.3 52.1 %collective-permute-start.4 = (bf16[784,512]{1,0:T(8,128)(2,1)}, bf16[784,512]{1,0:T(8,128)(2,1)}, u32[]{:S(2)}, u32[]{:S(2)}) collective-permute-start(bf16[784,512]{1,0:T(8,128)(2,1)} %collective-permute-done.2), channel_id=1, source_target_pairs={{0,1},{1,2},{2,3},{3,4},{4,5},{5,6},{6,7},{7,0},{8,9},{9,10},{10,1... | collective-permute-start | bytes 2408456 | tf_op jit(solution)/shard_map/ppermute | solution.py:219
  514.2 58.1 %collective-permute-start.5 = (bf16[784,512]{1,0:T(8,128)(2,1)}, bf16[784,512]{1,0:T(8,128)(2,1)}, u32[]{:S(2)}, u32[]{:S(2)}) collective-permute-start(bf16[784,512]{1,0:T(8,128)(2,1)} %collective-permute-done.3), channel_id=1, source_target_pairs={{0,7},{1,0},{2,1},{3,2},{4,3},{5,4},{6,5},{7,6},{8,15},{9,8},{10,9... | collective-permute-start | bytes 2408456 | tf_op jit(solution)/shard_map/ppermute | solution.py:224
  559.4 33.2 %collective-permute-start.6 = (bf16[784,512]{1,0:T(8,128)(2,1)}, bf16[784,512]{1,0:T(8,128)(2,1)}, u32[]{:S(2)}, u32[]{:S(2)}) collective-permute-start(bf16[784,512]{1,0:T(8,128)(2,1)} %collective-permute-done.4), channel_id=1, source_target_pairs={{0,1},{1,2},{2,3},{3,4},{4,5},{5,6},{6,7},{7,0},{8,9},{9,10},{10,1... | collective-permute-start | bytes 2408456 | tf_op jit(solution)/shard_map/ppermute | solution.py:219
  562.9 31.8 %copy-start.28 = (bf16[512,256]{1,0:T(8,128)(2,1)}, bf16[512,256]{1,0:T(8,128)(2,1)S(1)}, u32[]{:S(2)}) copy-start(bf16[512,256]{1,0:T(8,128)(2,1)S(1)} %squeeze_reshape.22) | copy-start | bytes 786436
  601.3 8.0 copy-start.29
  614.0 243.4 %reduce-scatter.9.cloned.1.call-start = ((), (), s32[]{:S(2)}) async-start(), calls=%async_computation.6 | async-start | bytes 7225344 | tf_op jit(solution)/shard_map/reduce_scatter | solution.py:285
  620.8 236.6 %copy-start.50 = (f32[1,512]{1,0:T(1,128)S(1)}, f32[1,512]{1,0:T(1,128)}, u32[]{:S(2)}) copy-start(f32[1,512]{1,0:T(1,128)} %get-tuple-element.47) | copy-start | bytes 6148
  620.8 341.9 %all-gather.9.cloned.1.call-start = ((), (), s32[]{:S(2)}) async-start(), calls=%async_computation.9 | async-start | bytes 7225344 | tf_op jit(solution)/shard_map/all_gather | solution.py:309
  863.2 367.9 %reduce-scatter.13.cloned.1.call-start = ((), (), s32[]{:S(2)}) async-start(), calls=%async_computation.10 | async-start | bytes 7225344 | tf_op jit(solution)/shard_map/reduce_scatter | solution.py:322
  879.9 82.8 %copy-start.30 = (bf16[64,512]{1,0:T(8,128)(2,1)S(1)}, bf16[64,512]{1,0:T(8,128)(2,1)}, u32[]{:S(2)}) copy-start(bf16[64,512]{1,0:T(8,128)(2,1)} %squeeze_reshape.21) | copy-start | bytes 196612
  974.8 8.8 copy-start.19
  974.8 8.8 copy-start.23
  974.8 16.7 %slice-start = ((s8[7340032]{0:T(1024)(128)(4,1)}), s8[3145728]{0:T(1024)(128)(4,1)S(1)}, s32[]{:S(2)}) async-start(s8[7340032]{0:T(1024)(128)(4,1)} %bitcast.149), calls=%async_computation.13 | async-start | bytes 6291456
  983.6 7.9 slice-start.1
  983.6 7.9 copy-start.10
  983.6 7.9 copy-start.11
  1113.1 211.7 %all-reduce.8.cloned.1.call-start = ((), (), s32[]{:S(2)}) async-start(), calls=%async_computation.12 | async-start | bytes 3154944
  1138.0 26.1 %copy-start.31 = (f32[1,1,64,512]{3,1,2,0:T(1,128)S(1)}, f32[1,1,64,512]{3,1,2,0:T(1,128)}, u32[]{:S(2)}) copy-start(f32[1,1,64,512]{3,1,2,0:T(1,128)} %copy.126) | copy-start | bytes 393220
  1163.9 69.8 %copy-start.48 = (f32[1,8,64]{2,1,0:T(8,128)S(1)}, f32[1,8,64]{2,1,0:T(8,128)}, u32[]{:S(2)}) copy-start(f32[1,8,64]{2,1,0:T(8,128)} %stack.47) | copy-start | bytes 6148
  1163.9 69.7 %copy-start.46 = (f32[1,8,64]{2,1,0:T(8,128)S(1)}, f32[1,8,64]{2,1,0:T(8,128)}, u32[]{:S(2)}) copy-start(f32[1,8,64]{2,1,0:T(8,128)} %stack.48) | copy-start | bytes 6148
  1163.9 69.8 %copy-start.47 = (f32[1,8,64]{2,1,0:T(8,128)S(1)}, f32[1,8,64]{2,1,0:T(8,128)}, u32[]{:S(2)}) copy-start(f32[1,8,64]{2,1,0:T(8,128)} %stack.49) | copy-start | bytes 6148
  1163.9 69.8 %copy-start.45 = (f32[1,8,64]{2,1,0:T(8,128)S(1)}, f32[1,8,64]{2,1,0:T(8,128)}, u32[]{:S(2)}) copy-start(f32[1,8,64]{2,1,0:T(8,128)} %stack.50) | copy-start | bytes 6148
  1163.9 115.0 %copy-start.54 = (f32[256]{0:T(256)S(1)}, f32[256]{0:T(256)}, u32[]{:S(2)}) copy-start(f32[256]{0:T(256)} %get-tuple-element.61) | copy-start | bytes 3076
  1163.9 121.0 %copy-start.14 = (f32[784,512]{1,0:T(8,128)S(1)}, f32[784,512]{1,0:T(8,128)}, u32[]{:S(2)}) copy-start(f32[784,512]{1,0:T(8,128)} %copy-done.13) | copy-start | bytes 4816900
  1231.1 53.8 %copy-start.20 = (bf16[784,512]{1,0:T(8,128)(2,1)S(1)}, bf16[784,512]{1,0:T(8,128)(2,1)}, u32[]{:S(2)}) copy-start(bf16[784,512]{1,0:T(8,128)(2,1)} %reduce-scatter.13.cloned.1.call-done) | copy-start | bytes 2408452
  1233.5 91.3 %copy-start.27 = (f32[1,98581]{1,0:T(1,128)S(1)}, f32[1,98581]{1,0:T(1,128)}, u32[]{:S(2)}) copy-start(f32[1,98581]{1,0:T(1,128)} %param.10) | copy-start | bytes 1182976
  1233.5 91.3 %copy-start.32 = (f32[1,98581]{1,0:T(1,128)S(1)}, f32[1,98581]{1,0:T(1,128)}, u32[]{:S(2)}) copy-start(f32[1,98581]{1,0:T(1,128)} %param.11) | copy-start | bytes 1182976
  (30 other events, 123.4 us)
Sparse Core Ops, SparseCore 0:
  15.3 37.3 all-reduce.5
  1284.3 40.4 all-reduce.7
Sparse Core Ops, SparseCore 1:
  17.8 103.1 all-gather.4
  285.9 118.0 reduce-scatter.6
  406.1 186.8 all-gather.6
  614.1 120.5 reduce-scatter.10
  738.3 119.0 reduce-scatter.8
  863.3 99.4 all-gather.8
  1113.2 117.9 reduce-scatter.12
